TPU v7x, 32 devices: a whole 2x2x4 slice. The times are simulated.
32 devices in a mesh: dp: 8 (over y, x, core), expert: 4 (over z).
Axes of the slice: x: 2, y: 2, z: 4, core: 2. Of those that a mesh axis runs over, the one named last changes fastest.
Arguments:
- policy_hidden: bfloat16 [1024, 4096], P('dp', 'expert'), may hold values from -6 to 6
- reference_hidden: bfloat16 [1024, 4096], P('dp', 'expert'), may hold values from -6 to 6
- policy_norm_gain: float32 [4096], P('expert'), may hold values from 0.25 to 1.75
- reference_norm_gain: float32 [4096], P('expert'), may hold values from 0.25 to 1.75
- policy_router: float32 [4096, 4], P('expert'), may hold values from -5.1875 to 5.1875
- reference_router: float32 [4096, 4], P('expert'), may hold values from -5.1875 to 5.1875
- policy_gate: bfloat16 [4, 4096, 8192], P('expert', 'dp'), may hold values from -0.09375 to 0.09375
- policy_up: bfloat16 [4, 4096, 8192], P('expert', 'dp'), may hold values from -0.09375 to 0.09375
- policy_down: bfloat16 [4, 8192, 4096], P('expert', 'dp'), may hold values from -0.0625 to 0.0625
- reference_gate: bfloat16 [4, 4096, 8192], P('expert', 'dp'), may hold values from -0.09375 to 0.09375
- reference_up: bfloat16 [4, 4096, 8192], P('expert', 'dp'), may hold values from -0.09375 to 0.09375
- reference_down: bfloat16 [4, 8192, 4096], P('expert', 'dp'), may hold values from -0.0625 to 0.0625
- expert_ids: int32 [1024, 2], P('dp'), may hold values from 0 to 3, all different within a row; in each aligned block of 128 rows (0 to 127, 128 to 255, ...) at most 96 rows name the same one
- lengths: int32 [32], P('dp'), may hold values from 1 to 32, as said below
Outputs:
- policy_mixture: bfloat16 [1024, 4096], P('dp', 'expert')
- reference_mixture: bfloat16 [1024, 4096], P('dp', 'expert')
- token_kl: float32 [1024], P('dp')
- loss: float32 [], replicated
Inputs may be any that keep to these rules, and one draw needn't show every extreme that they name: `expert_ids`: each row names 2 different experts; among the rows of one index of dp (aligned blocks of 128 rows) no expert is named more than 96 times, and in some block one expert is named exactly 96 times. The first lengths[r] of rollout r's 32 positions are live.
All inputs are finite; a program needn't handle non-finite values.
Results may differ from a plain program's by a relative error of at most 0.02.
Values may be sent and summed in bfloat16 or wider, within the bound.
A program may use at most 256 MiB of HBM per device.

v0:
```python
import jax
import jax.numpy as jnp
from jax import lax
from jax.sharding import PartitionSpec as P

D = 4096
SEG = 32


EPSILON = 1e-05
KL_WEIGHT = 1.0
BALANCE_WEIGHT = 0.5


def router_terms(hidden, norm_gain, router):
    values = hidden.astype(jnp.float32)
    partial_logits = jnp.dot(values * norm_gain, router, precision=lax.Precision.HIGHEST)
    return (partial_logits, jnp.sum(values * values, axis=1))


def expert_terms(slice_rows, weights):
    results = []
    for model_index in range(len(weights)):
        gate_weight, up_weight, down_weight = weights[model_index]
        model_rows = slice_rows[:, model_index, :]
        values = []
        for weight in (gate_weight, up_weight):
            partial = jnp.dot(model_rows, weight, preferred_element_type=jnp.float32)
            values.append(
                lax.psum_scatter(
                    partial.astype(jnp.bfloat16), "dp", scatter_dimension=1, tiled=True
                ).astype(jnp.float32)
            )
        hidden = (jax.nn.silu(values[0]) * values[1]).astype(jnp.bfloat16)
        partial = jnp.dot(hidden, down_weight, preferred_element_type=jnp.float32)
        results.append(
            lax.psum_scatter(
                partial.astype(jnp.bfloat16), "dp", scatter_dimension=0, tiled=True
            )
        )
    return jnp.stack(results, axis=1)


def mixture(slot_rows, weights):
    expert_count, slot_count, models, feature_block = slot_rows.shape
    model_width = expert_count * feature_block
    arrived_rows = lax.all_to_all(slot_rows, "expert", split_axis=0, concat_axis=3, tiled=True)
    local_rows = arrived_rows.reshape(slot_count, models, model_width)
    slice_rows = lax.all_to_all(local_rows, "dp", split_axis=2, concat_axis=0, tiled=True)
    summed = expert_terms(slice_rows, weights)
    result = lax.all_to_all(
        summed.reshape(1, slot_count, models, model_width),
        "expert",
        split_axis=3,
        concat_axis=0,
        tiled=True,
    )
    return result


def per_device(
    policy_hidden,
    reference_hidden,
    policy_norm_gain,
    reference_norm_gain,
    policy_router,
    reference_router,
    policy_gate,
    policy_up,
    policy_down,
    reference_gate,
    reference_up,
    reference_down,
    expert_ids,
    lengths,
):
    expert_count = lax.axis_size("expert")
    token_count, feature_block = policy_hidden.shape
    route_count = expert_ids.shape[1]
    slot_count = 3 * token_count // expert_count
    token_total = float(token_count * lax.axis_size("dp"))
    policy_partial, policy_squares = router_terms(policy_hidden, policy_norm_gain, policy_router)
    reference_partial, reference_squares = router_terms(
        reference_hidden, reference_norm_gain, reference_router
    )
    policy_partial, reference_partial, policy_squares, reference_squares = lax.psum(
        (policy_partial, reference_partial, policy_squares, reference_squares), "expert"
    )
    policy_scale = lax.rsqrt(policy_squares / D + EPSILON)[:, None]
    reference_scale = lax.rsqrt(reference_squares / D + EPSILON)[:, None]
    policy_logits = policy_partial * policy_scale
    reference_logits = reference_partial * reference_scale
    policy_rows = (policy_hidden.astype(jnp.float32) * policy_norm_gain * policy_scale).astype(
        jnp.bfloat16
    )
    reference_rows = (
        reference_hidden.astype(jnp.float32) * reference_norm_gain * reference_scale
    ).astype(jnp.bfloat16)
    live_mask = (
        (jnp.arange(SEG, dtype=jnp.int32)[None, :] < lengths[:, None])
        .reshape(-1)
        .astype(jnp.float32)
    )
    flat_ids = expert_ids.reshape(-1)
    onehot = (flat_ids[:, None] == jnp.arange(expert_count, dtype=jnp.int32)[None, :]).astype(
        jnp.int32
    )
    before = jnp.cumsum(onehot, axis=0) - onehot
    target = flat_ids * slot_count + jnp.sum(before * onehot, axis=1)
    slot_index = jnp.arange(expert_count * slot_count, dtype=jnp.int32)
    select = jnp.any(
        slot_index[:, None, None] == target.reshape(token_count, route_count)[None, :, :], axis=2
    ).astype(jnp.bfloat16)

    def pair_gates(logits):
        matches = expert_ids[:, :, None] == jnp.arange(expert_count, dtype=jnp.int32)[None, None, :]
        chosen = jnp.sum(jnp.where(matches, logits[:, None, :], 0.0), axis=2)
        return jax.nn.softmax(chosen, axis=1)

    def combine(expert_output, gates):
        picked = jnp.take(
            expert_output.reshape(expert_count * slot_count, feature_block), target, axis=0
        )
        picked = picked.reshape(token_count, route_count, feature_block).astype(jnp.float32)
        mixed_rows = jnp.sum(picked * gates[:, :, None], axis=1) * live_mask[:, None]
        return mixed_rows.astype(jnp.bfloat16)

    stacked_rows = jnp.concatenate((policy_rows, reference_rows), axis=1)
    placed = jnp.dot(select, stacked_rows, preferred_element_type=jnp.float32).astype(jnp.bfloat16)
    expert_output = mixture(
        placed.reshape(expert_count, slot_count, 2, feature_block),
        (
            (policy_gate[0], policy_up[0], policy_down[0]),
            (reference_gate[0], reference_up[0], reference_down[0]),
        ),
    )
    policy_output = expert_output[:, :, 0, :]
    reference_output = expert_output[:, :, 1, :]
    policy_mixture = combine(policy_output, pair_gates(policy_logits))
    reference_mixture = combine(reference_output, pair_gates(reference_logits))
    policy_logprob = jax.nn.log_softmax(policy_logits, axis=1)
    reference_logprob = jax.nn.log_softmax(reference_logits, axis=1)
    policy_prob = jnp.exp(policy_logprob)
    token_kl = jnp.sum(policy_prob * (policy_logprob - reference_logprob), axis=1) * live_mask
    route_onehot = onehot.reshape(token_count, route_count, expert_count)
    counts = jnp.sum(jnp.sum(route_onehot, axis=1).astype(jnp.float32) * live_mask[:, None], axis=0)
    probsum = jnp.sum(policy_prob * live_mask[:, None], axis=0)
    counts, probsum, kl_total = lax.psum((counts, probsum, jnp.sum(token_kl)), "dp")
    balance = expert_count * jnp.sum(counts / (route_count * token_total) * probsum / token_total)
    loss = KL_WEIGHT * kl_total / token_total + BALANCE_WEIGHT * balance
    return (policy_mixture, reference_mixture, token_kl, loss)


def solution(mesh):
    in_specs = (
        P("dp", "expert"),
        P("dp", "expert"),
        P("expert"),
        P("expert"),
        P("expert", None),
        P("expert", None),
        P("expert", "dp", None),
        P("expert", "dp", None),
        P("expert", "dp", None),
        P("expert", "dp", None),
        P("expert", "dp", None),
        P("expert", "dp", None),
        P("dp", None),
        P("dp"),
    )
    out_specs = (P("dp", "expert"), P("dp", "expert"), P("dp"), P())
    return jax.shard_map(
        per_device, mesh=mesh, in_specs=in_specs, out_specs=out_specs, check_vma=False
    )
```

profile of v0, /device:TPU:0, one launch (start us, length us, event | category | flops | bytes accessed | tf_op | source)
XLA Modules:
  0.0 709.4 jit_solution(10029497235971331076)
XLA Ops:
  10.5 1.5 fusion.28
  11.9 1.5 fusion.30
  13.4 13.7 %all-reduce.1 = (f32[128]{0:T(128)S(1)}, f32[128]{0:T(128)S(1)}, f32[128,4]{0,1:T(4,128)S(1)}, f32[128,4]{0,1:T(4,128)S(1)}) all-reduce(f32[128]{0:T(128)S(1)} %fusion.35, f32[128]{0:T(128)S(1)} %fusion.34, f32[128,4]{0,1:T(4,128)S(1)} %fusion.30, f32[128,4]{0,1:T(4,128)S(1)} %fusion.28), channel_id=1, replica_groups=mesh['dp'=8,'expert'=4] {'expert'}, use_global_device_ids=true, to_apply=%region_7.8 | all-reduce | flops 1280 | bytes 10240 | tf_op jit(solution)/shard_map/psum | solution.py:86
  29.3 1.2 reduce-window.6
  32.5 1.2 reshape.166
  34.1 38.3 %all_to_all.51 = bf16[4,96,2,1024]{3,1,2,0:T(8,128)(2,1)} all-to-all(bf16[4,96,2,1024]{3,1,2,0:T(8,128)(2,1)S(1)} %copy.90), channel_id=1, replica_groups=mesh['dp'=8,'expert'=4] {'expert'}, dimensions={0} | all-to-all | bytes 3145728 | tf_op jit(solution)/shard_map/all_to_all | solution.py:47
  72.4 4.6 copy.99
  77.0 30.2 %all_to_all.52 = bf16[96,2,4096]{0,1,2:T(2,128)(2,1)} all-to-all(bf16[96,2,4096]{0,1,2:T(2,128)(2,1)S(1)} %bitcast.74), channel_id=1, replica_groups=mesh['dp'=8,'expert'=4] {'dp'}, dimensions={2} | all-to-all | bytes 3145728 | tf_op jit(solution)/shard_map/all_to_all | solution.py:49
  107.2 4.7 copy.101
  111.9 13.0 %convolution_convert_fusion.3 = bf16[768,8192]{1,0:T(8,128)(2,1)} fusion(bf16[1,512,8192]{2,1,0:T(8,128)(2,1)} %param.23, bf16[768,2,512]{2,0,1:T(8,128)(2,1)S(1)} %bitcast.78), kind=kOutput, calls=%fused_computation.5 | convolution fusion | flops 6448742400 | bytes 21757952 | tf_op jit(solution)/shard_map/dot_general | solution.py:28
  124.9 15.1 %convolution_convert_fusion.2 = bf16[768,8192]{1,0:T(8,128)(2,1)} fusion(bf16[1,512,8192]{2,1,0:T(8,128)(2,1)} %param.24, bf16[768,2,512]{2,0,1:T(8,128)(2,1)S(1)} %bitcast.79), kind=kOutput, calls=%fused_computation.4 | convolution fusion | flops 6448742400 | bytes 21757952 | tf_op jit(solution)/shard_map/dot_general | solution.py:28
  140.2 13.3 %convolution_convert_fusion.1 = bf16[768,8192]{1,0:T(8,128)(2,1)} fusion(bf16[1,512,8192]{2,1,0:T(8,128)(2,1)} %param.26, bf16[768,2,512]{2,0,1:T(8,128)(2,1)S(1)} %bitcast.80), kind=kOutput, calls=%fused_computation.3 | convolution fusion | flops 6448742400 | bytes 21757952 | tf_op jit(solution)/shard_map/dot_general | solution.py:28
  153.7 12.9 %convolution_convert_fusion = bf16[768,8192]{1,0:T(8,128)(2,1)} fusion(bf16[1,512,8192]{2,1,0:T(8,128)(2,1)} %param.27, bf16[768,2,512]{2,0,1:T(8,128)(2,1)S(1)} %bitcast.81), kind=kOutput, calls=%fused_computation.2 | convolution fusion | flops 6448742400 | bytes 21757952 | tf_op jit(solution)/shard_map/dot_general | solution.py:28
  166.6 47.6 %reduce-scatter.7.cloned.1.call-done = bf16[768,1024]{1,0:T(8,128)(2,1)} async-done(((bf16[768,8192]{1,0:T(8,128)(2,1)}), bf16[768,1024]{1,0:T(8,128)(2,1)}) %reduce-scatter.7.cloned.1.call-update) | async-done | bytes 1572880 | tf_op jit(solution)/shard_map/reduce_scatter | solution.py:30
  214.2 95.5 %reduce-scatter.9.cloned.1.call-done = bf16[768,1024]{1,0:T(8,128)(2,1)} async-done(((bf16[768,8192]{1,0:T(8,128)(2,1)}), bf16[768,1024]{1,0:T(8,128)(2,1)}) %reduce-scatter.9.cloned.1.call-update) | async-done | bytes 1572880 | tf_op jit(solution)/shard_map/reduce_scatter | solution.py:30
  309.7 13.1 %fusion.8 = bf16[768,4096]{1,0:T(8,128)(2,1)} fusion(bf16[1,1024,4096]{2,1,0:T(8,128)(2,1)} %param.25, bf16[768,1024]{1,0:T(8,128)(2,1)} %reduce-scatter.9.cloned.1.call-done, bf16[768,1024]{1,0:T(8,128)(2,1)} %reduce-scatter.7.cloned.1.call-done), kind=kOutput, calls=%fused_computation.14 | convolution fusion | flops 6451888128 | bytes 17825792 | tf_op jit(solution)/shard_map/dot_general | solution.py:35
  322.9 82.3 %reduce-scatter.13.cloned.1.call-done = bf16[768,1024]{1,0:T(8,128)(2,1)} async-done(((bf16[768,8192]{1,0:T(8,128)(2,1)}), bf16[768,1024]{1,0:T(8,128)(2,1)}) %reduce-scatter.13.cloned.1.call-update) | async-done | bytes 1572880 | tf_op jit(solution)/shard_map/reduce_scatter | solution.py:30
  405.3 95.4 %reduce-scatter.15.cloned.1.call-done = bf16[768,1024]{1,0:T(8,128)(2,1)} async-done(((bf16[768,8192]{1,0:T(8,128)(2,1)}), bf16[768,1024]{1,0:T(8,128)(2,1)}) %reduce-scatter.15.cloned.1.call-update) | async-done | bytes 1572880 | tf_op jit(solution)/shard_map/reduce_scatter | solution.py:30
  500.6 12.7 %fusion.11 = bf16[768,4096]{1,0:T(8,128)(2,1)} fusion(bf16[1,1024,4096]{2,1,0:T(8,128)(2,1)} %param.28, bf16[768,1024]{1,0:T(8,128)(2,1)} %reduce-scatter.15.cloned.1.call-done, bf16[768,1024]{1,0:T(8,128)(2,1)} %reduce-scatter.13.cloned.1.call-done), kind=kOutput, calls=%fused_computation.15 | convolution fusion | flops 6451888128 | bytes 17825792 | tf_op jit(solution)/shard_map/dot_general | solution.py:35
  513.4 52.2 %reduce-scatter.11.cloned.1.call-done = bf16[96,4096]{1,0:T(8,128)(2,1)} async-done(((bf16[768,4096]{1,0:T(8,128)(2,1)}), bf16[96,4096]{1,0:T(8,128)(2,1)}) %reduce-scatter.11.cloned.1.call-update) | async-done | bytes 786448 | tf_op jit(solution)/shard_map/reduce_scatter | solution.py:37
  565.6 65.0 %reduce-scatter.17.cloned.1.call-done = bf16[96,4096]{1,0:T(8,128)(2,1)} async-done(((bf16[768,4096]{1,0:T(8,128)(2,1)}), bf16[96,4096]{1,0:T(8,128)(2,1)}) %reduce-scatter.17.cloned.1.call-update) | async-done | bytes 786448 | tf_op jit(solution)/shard_map/reduce_scatter | solution.py:37
  630.6 1.5 maximum_bitcast_fusion
  632.2 4.0 copy.95
  636.1 4.6 all-to-all-start.2
  642.3 13.7 %all-reduce = (f32[]{:T(128)}, f32[4]{0:T(128)S(1)}, f32[4]{0:T(128)S(1)}) all-reduce(f32[]{:T(128)} %get-tuple-element.18, f32[4]{0:T(128)S(1)} %get-tuple-element.6, f32[4]{0:T(128)S(1)} %get-tuple-element.10), channel_id=1, replica_groups=mesh['dp'=8,'expert'=4] {'dp'}, use_global_device_ids=true, to_apply=%region_28.31 | all-reduce | flops 9 | bytes 72 | tf_op jit(solution)/shard_map/psum | solution.py:148
  658.3 30.5 %all-to-all-done.2 = bf16[1,96,2,4096]{1,2,0,3:T(2,128)(2,1)S(1)} async-done(((bf16[1,96,2,4096]{1,2,0,3:T(2,128)(2,1)}), bf16[1,96,2,4096]{1,2,0,3:T(2,128)(2,1)S(1)}, u32[]{:S(2)}, u32[]{:S(2)}) %all-to-all-start.2) | async-done | bytes 1572896 | tf_op jit(solution)/shard_map/all_to_all | solution.py:51
  688.7 3.7 copy.96
  692.4 1.6 fusion.57
  694.0 1.2 gather_fusion
  695.2 1.2 gather_fusion.1
  697.8 1.3 multiply_reduce_fusion.1
  699.2 1.3 multiply_reduce_fusion
  (70 shorter events, 13.2 us)
Async XLA Ops:
  7.2 3.3 copy-start
  7.2 207.0 %reduce-scatter.7.cloned.1.call-start = ((), (), s32[]{:S(2)}) async-start(), calls=%async_computation.9 | async-start | bytes 14155776 | tf_op jit(solution)/shard_map/reduce_scatter | solution.py:30
  124.9 184.9 %reduce-scatter.9.cloned.1.call-start = ((), (), s32[]{:S(2)}) async-start(), calls=%async_computation.10 | async-start | bytes 14155776 | tf_op jit(solution)/shard_map/reduce_scatter | solution.py:30
  140.0 265.2 %reduce-scatter.13.cloned.1.call-start = ((), (), s32[]{:S(2)}) async-start(), calls=%async_computation.12 | async-start | bytes 14155776 | tf_op jit(solution)/shard_map/reduce_scatter | solution.py:30
  153.6 347.0 %reduce-scatter.15.cloned.1.call-start = ((), (), s32[]{:S(2)}) async-start(), calls=%async_computation.13 | async-start | bytes 14155776 | tf_op jit(solution)/shard_map/reduce_scatter | solution.py:30
  166.5 399.1 %reduce-scatter.11.cloned.1.call-start = ((), (), s32[]{:S(2)}) async-start(), calls=%async_computation.11 | async-start | bytes 7077888 | tf_op jit(solution)/shard_map/reduce_scatter | solution.py:37
  322.9 307.7 %reduce-scatter.17.cloned.1.call-start = ((), (), s32[]{:S(2)}) async-start(), calls=%async_computation.14 | async-start | bytes 7077888 | tf_op jit(solution)/shard_map/reduce_scatter | solution.py:37
  632.1 8.6 %copy-start.3 = (s32[4]{0:T(128)S(1)}, s32[4]{0:T(128)}, u32[]{:S(2)}) copy-start(s32[4]{0:T(128)} %param.30) | copy-start | bytes 52
  632.1 8.8 %copy-start.2 = (s32[128,2]{0,1:T(2,128)S(1)}, s32[128,2]{0,1:T(2,128)}, u32[]{:S(2)}) copy-start(s32[128,2]{0,1:T(2,128)} %param.29) | copy-start | bytes 3076
  636.1 52.6 %all-to-all-start.2 = ((bf16[1,96,2,4096]{1,2,0,3:T(2,128)(2,1)}), bf16[1,96,2,4096]{1,2,0,3:T(2,128)(2,1)S(1)}, u32[]{:S(2)}, u32[]{:S(2)}) async-start(bf16[1,96,2,4096]{1,2,0,3:T(2,128)(2,1)} %copy.95), calls=%async_computation.8 | async-start | bytes 4194304 | tf_op jit(solution)/shard_map/all_to_all | solution.py:51
  697.2 4.3 copy-start.1
Sparse Core Ops, SparseCore 0:
  125.0 89.1 reduce-scatter.6
  217.7 91.9 reduce-scatter.8
  313.2 91.9 reduce-scatter.12
  408.6 91.9 reduce-scatter.14
  503.8 61.7 reduce-scatter.10
  568.8 61.7 reduce-scatter.16
where the time goes:
time: 710 us; the launch traced here: 709 us
  waiting for transfers between devices  469 us (66%)
  blocking collectives  95.8 us (13%)
  matrix products  83.6 us (12%)
  local copies, waits for them, and re-layouts  25.6 us (4%)
  between operations  16.8 us (2%)
  other arithmetic  13.9 us (2%)
    reduce_scatter x4, waiting for transfers between devices, expert_terms(): lax.psum_scatter(partial.astype(jnp.bfloat16), 'dp', scatter_dimension=1,...  321 us
    reduce_scatter x2, waiting for transfers between devices, expert_terms(): lax.psum_scatter(partial.astype(jnp.bfloat16), 'dp', scatter_dimension=0,...  117 us
    dot_general x4, matrix products, expert_terms(): partial = jnp.dot(model_rows, weight, preferred_element_type=jnp.float32)  54.2 us
    all_to_all x1, blocking collectives, mixture(): lax.all_to_all(slot_rows, 'expert', split_axis=0, concat_axis=3, tiled=True)  38.3 us
    all_to_all x1, waiting for transfers between devices, mixture(): lax.all_to_all(summed.reshape(1, slot_count, models, model_width), 'exper...  30.5 us
    all_to_all x1, blocking collectives, mixture(): lax.all_to_all(local_rows, 'dp', split_axis=2, concat_axis=0, tiled=True)  30.2 us
    dot_general x2, matrix products, expert_terms(): partial = jnp.dot(hidden, down_weight, preferred_element_type=jnp.float32)  25.9 us
  transfers between devices with their start and end apart: 7, of which 7 were waited for; matrix products, arithmetic and copies ran while one was open for 10% of the time, Pallas kernels for 0%

commit v1 on v0

v1 whole, which is shorter than its diff:
```python
import functools

import jax
import jax.numpy as jnp
from jax import lax
from jax.experimental import pallas as pl
from jax.experimental.pallas import tpu as pltpu
from jax.sharding import PartitionSpec as P

D = 4096
SEG = 32

EPSILON = 1e-05
KL_WEIGHT = 1.0
BALANCE_WEIGHT = 0.5

MESH = pl.DeviceIdType.MESH
VMEM = pl.BlockSpec(memory_space=pltpu.VMEM)
ANY = pl.BlockSpec(memory_space=pl.ANY)
VMEM_LIMIT = 67043328


def remote(src, dst, send_sem, recv_sem, dp, expert):
    return pltpu.make_async_remote_copy(
        src_ref=src,
        dst_ref=dst,
        send_sem=send_sem,
        recv_sem=recv_sem,
        device_id=(dp, expert),
        device_id_type=MESH,
    )


def greet(peers):
    barrier = pltpu.get_barrier_semaphore()
    for peer in peers:
        pl.semaphore_signal(barrier, inc=1, device_id=peer, device_id_type=MESH)
    pl.semaphore_wait(barrier, len(peers))


def around(index, size):
    return [lax.rem(index + step, size) for step in range(1, size)]


def small_kernel(n, z, terms_ref, counts_ref, all_terms, all_counts, sems):
    dp, ex = lax.axis_index("dp"), lax.axis_index("expert")
    ex_peers, dp_peers = around(ex, z), around(dp, n)
    greet([(dp, peer) for peer in ex_peers] + [(peer, ex) for peer in dp_peers])
    copies = []
    for step, peer in enumerate(dp_peers):
        copies.append(
            remote(counts_ref, all_counts.at[dp], sems.at[0, step], sems.at[1, step], peer, ex)
        )
    for step, peer in enumerate(ex_peers):
        at = n - 1 + step
        copies.append(
            remote(terms_ref, all_terms.at[ex], sems.at[0, at], sems.at[1, at], dp, peer)
        )
    for copy in copies:
        copy.start()
    all_counts[dp] = counts_ref[...]
    all_terms[ex] = terms_ref[...]
    for copy in copies:
        copy.wait()


def small_exchange(n, z, terms, counts):
    return pl.pallas_call(
        functools.partial(small_kernel, n, z),
        out_shape=(
            jax.ShapeDtypeStruct((z,) + terms.shape, terms.dtype),
            jax.ShapeDtypeStruct((n,) + counts.shape, counts.dtype),
        ),
        in_specs=[VMEM] * 2,
        out_specs=(VMEM,) * 2,
        scratch_shapes=[pltpu.SemaphoreType.DMA((2, n + z - 2))],
        compiler_params=pltpu.CompilerParams(collective_id=0, has_side_effects=True),
        name="small_exchange",
    )(terms, counts)


def entry_kernel(n, z, placed, out, relay, send_one, recv_one, send_two, recv_two):
    dp, ex = lax.axis_index("dp"), lax.axis_index("expert")
    halves = n // z
    cap, width = relay.shape[2], relay.shape[3]
    ex_peers, dp_peers = around(ex, z), around(dp, n)
    greet([(dp, peer) for peer in ex_peers] + [(peer, ex) for peer in dp_peers])

    def slots(expert, model, half):
        rows = pl.ds(pl.multiple_of(expert * cap, cap), cap)
        return placed.at[rows, pl.ds((model * halves + half) * width, width)]

    def landing(model, block):
        return out.at[model, pl.ds(pl.multiple_of(block * cap, cap), cap), :]

    first = []
    for model in range(2):
        for step, peer in enumerate(ex_peers):
            for half in range(halves):
                copy = remote(
                    slots(peer, model, half),
                    relay.at[model, ex * halves + half],
                    send_one.at[model, step, half],
                    recv_one.at[model, ex * halves + half],
                    dp,
                    peer,
                )
                copy.start()
                first.append(copy)

    def second(model, block, source):
        return remote(
            source,
            landing(model, dp),
            send_two.at[model, block],
            recv_two.at[model, dp],
            block,
            ex,
        )

    def forward(model, block, source):
        @pl.when(block != dp)
        def _():
            second(model, block, source).start()

        @pl.when(block == dp)
        def _():
            landing(model, dp)[...] = source[...]

    for model in range(2):
        for half in range(halves):
            forward(model, ex * halves + half, slots(ex, model, half))
        for step, peer in enumerate(reversed(ex_peers)):
            for half in range(halves):
                block = peer * halves + half
                remote(
                    relay.at[model, block],
                    relay.at[model, block],
                    send_one.at[model, 0, half],
                    recv_one.at[model, block],
                    dp,
                    peer,
                ).wait_recv()
                forward(model, block, relay.at[model, block])
    for model in range(2):
        for peer in dp_peers:
            remote(
                landing(model, peer),
                landing(model, peer),
                send_two.at[model, peer],
                recv_two.at[model, peer],
                peer,
                ex,
            ).wait_recv()
            second(model, peer, relay.at[model, peer]).wait_send()
    for copy in first:
        copy.wait_send()


def entry_exchange(n, z, cap, width, placed):
    halves = n // z
    return pl.pallas_call(
        functools.partial(entry_kernel, n, z),
        out_shape=jax.ShapeDtypeStruct((2, n * cap, width), placed.dtype),
        in_specs=[VMEM],
        out_specs=VMEM,
        scratch_shapes=[
            pltpu.VMEM((2, n, cap, width), placed.dtype),
            pltpu.SemaphoreType.DMA((2, z - 1, halves)),
            pltpu.SemaphoreType.DMA((2, n)),
            pltpu.SemaphoreType.DMA((2, n)),
            pltpu.SemaphoreType.DMA((2, n)),
        ],
        compiler_params=pltpu.CompilerParams(collective_id=1, has_side_effects=True),
        name="entry_exchange",
    )(placed)


def exit_kernel(
    n, z, rows_ref, stats_ref, out, all_stats, relay, send_one, recv_one, send_two, recv_two, sems
):
    dp, ex = lax.axis_index("dp"), lax.axis_index("expert")
    halves = n // z
    cap, width = relay.shape[2], relay.shape[3]
    ex_peers, dp_peers = around(ex, z), around(dp, n)
    greet([(dp, peer) for peer in ex_peers] + [(peer, ex) for peer in dp_peers])

    def source(model, block):
        return rows_ref.at[model, pl.ds(pl.multiple_of(block * cap, cap), cap), :]

    def landing(model, expert, half):
        rows = pl.ds(pl.multiple_of(expert * cap, cap), cap)
        return out.at[model, rows, pl.ds(pl.multiple_of(half * width, width), width)]

    stats = []
    for step, peer in enumerate(dp_peers):
        copy = remote(stats_ref, all_stats.at[dp], sems.at[0, step], sems.at[1, step], peer, ex)
        copy.start()
        stats.append(copy)
    first = []
    for model in range(2):
        for step, peer in enumerate(dp_peers):
            copy = remote(
                source(model, peer),
                relay.at[model, dp],
                send_one.at[model, step],
                recv_one.at[model, dp],
                peer,
                ex,
            )
            copy.start()
            first.append(copy)
    all_stats[dp] = stats_ref[...]

    def second(model, block, origin):
        return remote(
            origin,
            landing(model, ex, lax.rem(block, halves)),
            send_two.at[model, block],
            recv_two.at[model, ex, lax.rem(block, halves)],
            dp,
            block // halves,
        )

    def forward(model, block, origin):
        @pl.when(block // halves != ex)
        def _():
            second(model, block, origin).start()

        @pl.when(block // halves == ex)
        def _():
            landing(model, ex, lax.rem(block, halves))[...] = origin[...]

    for model in range(2):
        forward(model, dp, source(model, dp))
        for peer in reversed(dp_peers):
            remote(
                relay.at[model, peer],
                relay.at[model, peer],
                send_one.at[model, 0],
                recv_one.at[model, peer],
                peer,
                ex,
            ).wait_recv()
            forward(model, peer, relay.at[model, peer])
    for model in range(2):
        for peer in ex_peers:
            for half in range(halves):
                remote(
                    landing(model, peer, half),
                    landing(model, peer, half),
                    send_two.at[model, peer * halves + half],
                    recv_two.at[model, peer, half],
                    dp,
                    peer,
                ).wait_recv()
                second(
                    model, peer * halves + half, relay.at[model, peer * halves + half]
                ).wait_send()
    for copy in first:
        copy.wait_send()
    for copy in stats:
        copy.wait()


def exit_exchange(n, z, cap, width, rows, stats):
    halves = n // z
    return pl.pallas_call(
        functools.partial(exit_kernel, n, z),
        out_shape=(
            jax.ShapeDtypeStruct((2, z * cap, halves * width), rows.dtype),
            jax.ShapeDtypeStruct((n,) + stats.shape, stats.dtype),
        ),
        in_specs=[VMEM] * 2,
        out_specs=(VMEM,) * 2,
        scratch_shapes=[
            pltpu.VMEM((2, n, cap, width), rows.dtype),
            pltpu.SemaphoreType.DMA((2, n - 1)),
            pltpu.SemaphoreType.DMA((2, n)),
            pltpu.SemaphoreType.DMA((2, n)),
            pltpu.SemaphoreType.DMA((2, z, halves)),
            pltpu.SemaphoreType.DMA((2, n - 1)),
        ],
        compiler_params=pltpu.CompilerParams(collective_id=2, has_side_effects=True),
        name="exit_exchange",
    )(rows, stats)


class Plan:
    def __init__(self, n, blocks_up, blocks_down):
        self.levels = n.bit_length() - 1
        self.lags = [0] + [2 * p - 1 for p in range(1, self.levels + 1)]
        last = self.lags[-1]
        self.gu = 2 * blocks_up
        self.dn = blocks_down
        self.down0 = self.gu - 1 + last
        self.rest = self.down0 + self.dn
        self.end = 2 * self.gu + self.dn
        self.down1 = self.end - 1 + last
        self.ids = self.down1 + self.dn
        self.units = self.end + self.dn
        self.steps = self.ids + last

    def is_gu(self, u):
        return ((u >= 0) & (u < self.down0)) | ((u >= self.rest) & (u < self.end))

    def is_dn(self, u):
        return ((u >= self.down0) & (u < self.rest)) | ((u >= self.down1) & (u < self.ids))

    def gu_at(self, u):
        index = jnp.where(u < self.down0, u, u - self.dn)
        inner = lax.rem(index, self.gu)
        return index // self.gu, inner // 2, lax.rem(inner, 2)

    def dn_at(self, u):
        late = u >= self.rest
        return jnp.where(late, 1, 0), jnp.where(late, u - self.down1, u - self.down0)

    def buffer(self, u):
        return jnp.where(u < self.end, u, u - (self.down1 - self.end))


def expert_kernel(n, plan, rows_ref, gate0, up0, down0, gate1, up1, down1, out_ref, *scratch):
    levels, lags = plan.levels, plan.lags
    sends, recvs, keeps = scratch[:levels], scratch[levels : 2 * levels], scratch[2 * levels : 3 * levels - 1]
    wide, tall, hidden, gated, wsem, ssem, rsem = scratch[3 * levels - 1 :]
    me, ex = lax.axis_index("dp"), lax.axis_index("expert")
    w = wide.shape[-1]
    depth, width = gate0.shape[0], down0.shape[0]
    send_slots, keep_slots = sends[0].shape[0], keeps[0].shape[0]

    def bit(stride):
        return lax.rem(me // stride, 2)

    def partner(stride):
        return me + stride * (1 - 2 * bit(stride))

    def tiles(half, u, ref, block, span, held):
        low = bit(1)
        parity = 1 - low if half == 0 else low
        slot = lax.rem(u, 2)
        for q in range(n // 2):
            start = pl.multiple_of((2 * q + parity) * span + block * w, w)
            yield pltpu.make_async_copy(
                ref.at[:, pl.ds(start, w)], held.at[half, slot, q], wsem.at[half, slot, q]
            )

    def fetch(half, u):
        model, block, which = plan.gu_at(u)
        for m, g, ref in ((0, 0, gate0), (0, 1, up0), (1, 0, gate1), (1, 1, up1)):

            @pl.when(plan.is_gu(u) & (model == m) & (which == g))
            def _():
                for copy in tiles(half, u, ref, block, width, wide):
                    copy.start()

        dn_model, dn_block = plan.dn_at(u)
        for m, ref in ((0, down0), (1, down1)):

            @pl.when(plan.is_dn(u) & (dn_model == m))
            def _():
                for copy in tiles(half, u, ref, dn_block, depth, tall):
                    copy.start()

    def arrived(half, u):
        for condition, ref, span, held in (
            (plan.is_gu(u), gate0, width, wide),
            (plan.is_dn(u), down0, depth, tall),
        ):

            @pl.when(condition)
            def _():
                for copy in tiles(half, u, ref, 0, span, held):
                    copy.wait()

    def gu_product(u, half, q):
        model, _, _ = plan.gu_at(u)
        return jnp.dot(
            rows_ref[model],
            wide[half, lax.rem(u, 2), q],
            preferred_element_type=jnp.float32,
        )

    def dn_product(u, half, q):
        model, _ = plan.dn_at(u)
        return jnp.dot(
            hidden[model],
            tall[half, lax.rem(u, 2), q],
            preferred_element_type=jnp.float32,
        )

    def placing(p, u):
        color = lax.rem(u, 2)
        one, two = bit(2**p), bit(2 ** (levels - p))
        mine = one + color * (two - one)
        top = 2 ** (levels - p - 1)

        def place(r, keep):
            value = mine if keep else 1 - mine
            return r * (2 - color) + value * (1 + color * (top - 1))

        return place

    def hop(p, u):
        color = lax.rem(u, 2)
        one, two = partner(2 ** p), partner(2 ** (levels - p) if p else 1)
        return remote(
            sends[p].at[lax.rem(u, send_slots)],
            recvs[p].at[plan.buffer(u)],
            ssem.at[p, lax.rem(u, send_slots)],
            rsem.at[p, plan.buffer(u)],
            one + color * (two - one),
            ex,
        )

    def level_zero(u):
        arrived(0, u)
        slot = lax.rem(u, send_slots)
        for condition, product in ((plan.is_gu(u), gu_product), (plan.is_dn(u), dn_product)):

            @pl.when(condition)
            def _():
                for q in range(n // 2):
                    sends[0][slot, q] = product(u, 0, q).astype(jnp.bfloat16)
                hop(0, u).start()

    def level_one(u):
        arrived(1, u)
        slot, kept, buffer = lax.rem(u, send_slots), lax.rem(u, keep_slots), plan.buffer(u)
        place = placing(1, u)
        for condition, product in ((plan.is_gu(u), gu_product), (plan.is_dn(u), dn_product)):

            @pl.when(condition)
            def _():
                hop(0, u).wait_recv()
                for keep in (False, True):
                    for r in range(n // 4):
                        at = place(r, keep)
                        total = product(u, 1, at) + recvs[0][buffer, at].astype(jnp.float32)
                        if keep:
                            keeps[0][kept, r] = total.astype(jnp.bfloat16)
                        else:
                            sends[1][slot, r] = total.astype(jnp.bfloat16)
                    if not keep:
                        hop(1, u).start()

    def level(p, u):
        slot, kept, buffer = lax.rem(u, send_slots), lax.rem(u, keep_slots), plan.buffer(u)
        place = placing(p, u)

        @pl.when(plan.is_gu(u) | plan.is_dn(u))
        def _():
            hop(p - 1, u).wait_recv()
            for keep in (False, True):
                for r in range(n // 2 ** (p + 1)):
                    at = place(r, keep)
                    total = keeps[p - 2][kept, at].astype(jnp.float32) + recvs[p - 1][
                        buffer, at
                    ].astype(jnp.float32)
                    if keep:
                        keeps[p - 1][kept, r] = total.astype(jnp.bfloat16)
                    else:
                        sends[p][slot, r] = total.astype(jnp.bfloat16)
                if not keep:
                    hop(p, u).start()

    def finish(u):
        kept, buffer = lax.rem(u, keep_slots), plan.buffer(u)

        def total():
            return keeps[-1][kept, 0].astype(jnp.float32) + recvs[-1][buffer, 0].astype(jnp.float32)

        @pl.when(plan.is_gu(u) | plan.is_dn(u))
        def _():
            hop(levels - 1, u).wait_recv()

        model, block, which = plan.gu_at(u)

        @pl.when(plan.is_gu(u) & (which == 0))
        def _():
            gated[...] = total()

        @pl.when(plan.is_gu(u) & (which == 1))
        def _():
            value = gated[...]
            hidden[model, :, pl.ds(pl.multiple_of(block * w, w), w)] = (
                value / (1.0 + jnp.exp(-value)) * total()
            ).astype(jnp.bfloat16)

        dn_model, dn_block = plan.dn_at(u)

        @pl.when(plan.is_dn(u))
        def _():
            out_ref[dn_model, :, pl.ds(pl.multiple_of(dn_block * w, w), w)] = total().astype(
                jnp.bfloat16
            )

        @pl.when(plan.is_gu(u) | plan.is_dn(u))
        def _():
            for p in range(levels):
                hop(p, u).wait_send()

    fetch(0, jnp.int32(0))
    greet([(partner(2**p), ex) for p in range(levels)])

    def step(t, carry):
        fetch(0, t + 1)
        fetch(1, t)
        finish(t - lags[levels])
        for p in range(levels - 1, 1, -1):
            level(p, t - lags[p])
        level_one(t - lags[1])
        level_zero(t)
        return carry

    lax.fori_loop(0, plan.steps, step, 0)


def experts(n, rows, weights):
    (gate0, up0, down0), (gate1, up1, down1) = weights
    _, chunk, depth = rows.shape
    width = down0.shape[0]
    w = depth // 2
    plan = Plan(n, width // w, depth // w)
    levels = plan.levels
    if 2**levels != n or levels < 2:
        raise ValueError("dp size")
    send_slots, keep_slots = plan.lags[-1] + 1, 4
    bf = jnp.bfloat16
    parts = [n // 2 ** (p + 1) for p in range(levels)]
    flops = 2 * chunk * 3 * depth * n * width * 2
    return pl.pallas_call(
        functools.partial(expert_kernel, n, plan),
        out_shape=jax.ShapeDtypeStruct((2, chunk, depth), bf),
        in_specs=[VMEM] + [ANY] * 6,
        out_specs=VMEM,
        scratch_shapes=[pltpu.VMEM((send_slots, part, chunk, w), bf) for part in parts]
        + [pltpu.VMEM((plan.units, part, chunk, w), bf) for part in parts]
        + [pltpu.VMEM((keep_slots, part, chunk, w), bf) for part in parts[1:]]
        + [
            pltpu.VMEM((2, 2, n // 2, depth, w), bf),
            pltpu.VMEM((2, 2, n // 2, width, w), bf),
            pltpu.VMEM((2, chunk, width), bf),
            pltpu.VMEM((chunk, w), jnp.float32),
            pltpu.SemaphoreType.DMA((2, 2, n // 2)),
            pltpu.SemaphoreType.DMA((levels, send_slots)),
            pltpu.SemaphoreType.DMA((levels, plan.units)),
        ],
        compiler_params=pltpu.CompilerParams(
            collective_id=3, has_side_effects=True, vmem_limit_bytes=VMEM_LIMIT
        ),
        cost_estimate=pl.CostEstimate(flops=flops, bytes_accessed=12 * depth * n * width, transcendentals=0),
        name="experts",
    )(rows, gate0, up0, down0, gate1, up1, down1)


def per_device(
    policy_hidden,
    reference_hidden,
    policy_norm_gain,
    reference_norm_gain,
    policy_router,
    reference_router,
    policy_gate,
    policy_up,
    policy_down,
    reference_gate,
    reference_up,
    reference_down,
    expert_ids,
    lengths,
):
    n, z = lax.axis_size("dp"), lax.axis_size("expert")
    ex = lax.axis_index("expert")
    tokens, features = policy_hidden.shape
    routes = expert_ids.shape[1]
    cap = 3 * tokens // z
    depth = policy_gate.shape[1]
    token_total = float(tokens * n)
    f32, bf = jnp.float32, jnp.bfloat16

    live = (jnp.arange(SEG, dtype=jnp.int32)[None, :] < lengths[:, None]).reshape(-1)
    live_f = live.astype(f32)
    flat_ids = expert_ids.reshape(-1)
    flat_live = jnp.repeat(live, routes)
    choice = flat_ids[:, None] == jnp.arange(z, dtype=jnp.int32)[None, :]
    onehot = (choice & flat_live[:, None]).astype(bf)
    order = jnp.arange(tokens * routes, dtype=jnp.int32)
    earlier = (order[None, :] < order[:, None]).astype(bf)
    before = jnp.dot(earlier, onehot, preferred_element_type=f32)
    pos = jnp.sum(before * choice.astype(f32), axis=1).astype(jnp.int32)
    target = jnp.where(flat_live, flat_ids * cap + pos, -1).reshape(tokens, routes)
    counts = jnp.sum(onehot.astype(f32), axis=0)
    counts_tile = jnp.pad(counts[None, :], ((0, 7), (0, 128 - z)))

    def router_terms(hidden, gain, router):
        values = hidden.astype(f32)
        logits = lax.dot_general(
            router, values * gain, (((0,), (1,)), ((), ())), precision=lax.Precision.HIGHEST
        )
        return jnp.concatenate((logits, jnp.sum(values * values, axis=1)[None, :]), axis=0)

    terms = jnp.concatenate(
        (
            router_terms(policy_hidden, policy_norm_gain, policy_router),
            router_terms(reference_hidden, reference_norm_gain, reference_router),
        ),
        axis=0,
    )
    terms = jnp.pad(terms, ((0, -terms.shape[0] % 8), (0, 0)))
    all_terms, all_counts = small_exchange(n, z, terms, counts_tile)
    terms = jnp.sum(all_terms, axis=0)
    block_counts = all_counts[:, 0, :z].astype(jnp.int32)

    def model_terms(base, hidden, gain):
        scale = lax.rsqrt(terms[base + z] / (n * depth) + EPSILON)
        logits = terms[base : base + z] * scale[None, :]
        rows = (hidden.astype(f32) * gain * scale[:, None]).astype(bf)
        return logits, rows

    policy_logits, policy_rows = model_terms(0, policy_hidden, policy_norm_gain)
    reference_logits, reference_rows = model_terms(z + 1, reference_hidden, reference_norm_gain)

    slot = jnp.arange(z * cap, dtype=jnp.int32)
    picks = [(target[:, k][:, None] == slot[None, :]).astype(bf) for k in range(routes)]
    select = sum(slot[:, None] == target[:, k][None, :] for k in range(routes)).astype(bf)
    stacked = jnp.concatenate((policy_rows, reference_rows), axis=1)
    placed = jnp.dot(select, stacked, preferred_element_type=f32).astype(bf)
    slot_rows = entry_exchange(n, z, cap, depth, placed)

    totals = jnp.sum(block_counts, axis=0)
    mine = lax.dynamic_slice_in_dim(block_counts, ex, 1, axis=1)[:, 0]
    first = jnp.cumsum(mine) - mine
    within = jnp.arange(cap, dtype=jnp.int32)
    packed = jnp.where(
        within[None, :] < mine[:, None], first[:, None] + within[None, :], -1
    ).reshape(-1)
    chunk = -(-5 * n * cap // 12 // 16) * 16
    weights = (
        (policy_gate[0], policy_up[0], policy_down[0]),
        (reference_gate[0], reference_up[0], reference_down[0]),
    )

    def body(index, results):
        wanted = index * chunk + jnp.arange(chunk, dtype=jnp.int32)
        gather = (wanted[:, None] == packed[None, :]).astype(bf)
        rows = lax.dot_general(
            slot_rows, gather, (((1,), (1,)), ((), ())), preferred_element_type=f32
        )
        rows = rows.astype(bf).transpose(0, 2, 1)
        outs = experts(n, rows, weights)
        spread = (packed[:, None] == wanted[None, :]).astype(bf)
        return results + jnp.einsum(
            "sr,mrd->msd", spread, outs, preferred_element_type=f32
        ).astype(bf)

    passes = (jnp.max(totals) + chunk - 1) // chunk
    results = lax.fori_loop(0, passes, body, jnp.zeros((2, n * cap, depth), bf))

    policy_logprob = jax.nn.log_softmax(policy_logits, axis=0)
    reference_logprob = jax.nn.log_softmax(reference_logits, axis=0)
    policy_prob = jnp.exp(policy_logprob)
    token_kl = jnp.sum(policy_prob * (policy_logprob - reference_logprob), axis=0) * live_f
    probsum = jnp.sum(policy_prob * live_f[None, :], axis=1)
    stats = jnp.concatenate((probsum, jnp.sum(token_kl)[None]))
    stats_tile = jnp.pad(stats[None, :], ((0, 7), (0, 128 - z - 1)))

    arrived, all_stats = exit_exchange(n, z, cap, depth, results, stats_tile)

    def combine(model, logits):
        matches = expert_ids[:, :, None] == jnp.arange(z, dtype=jnp.int32)[None, None, :]
        chosen = jnp.sum(jnp.where(matches, logits.T[:, None, :], 0.0), axis=2)
        gates = jax.nn.softmax(chosen, axis=1)
        total = 0.0
        for k in range(routes):
            picked = jnp.dot(picks[k], arrived[model], preferred_element_type=f32)
            total = total + picked * gates[:, k : k + 1]
        return (total * live_f[:, None]).astype(bf)

    policy_mixture = combine(0, policy_logits)
    reference_mixture = combine(1, reference_logits)
    stats = jnp.sum(all_stats[:, 0, :], axis=0)
    balance = z * jnp.sum(
        totals.astype(f32) / (routes * token_total) * stats[:z] / token_total
    )
    loss = KL_WEIGHT * stats[z] / token_total + BALANCE_WEIGHT * balance
    return (policy_mixture, reference_mixture, token_kl, loss)


def solution(mesh):
    in_specs = (
        P("dp", "expert"),
        P("dp", "expert"),
        P("expert"),
        P("expert"),
        P("expert", None),
        P("expert", None),
        P("expert", "dp", None),
        P("expert", "dp", None),
        P("expert", "dp", None),
        P("expert", "dp", None),
        P("expert", "dp", None),
        P("expert", "dp", None),
        P("dp", None),
        P("dp"),
    )
    out_specs = (P("dp", "expert"), P("dp", "expert"), P("dp"), P())
    return jax.shard_map(
        per_device, mesh=mesh, in_specs=in_specs, out_specs=out_specs, check_vma=False
    )
```

time: 710 us -> 274 us (0.39)
  waiting for transfers between devices: 469 us -> 0 us
  Pallas kernels: 0 us -> 229 us
  blocking collectives: 95.8 us -> 0 us
  matrix products: 83.6 us -> 16.2 us
  local copies, waits for them, and re-layouts: 25.6 us -> 10 us
  between operations: 16.8 us -> 4.08 us
    reduce_scatter x6 -> x0, waiting for transfers between devices: 438 us -> none  [the longest x4 321 us: expert_terms(): lax.psum_scatter(partial.astype(jnp.bfloat16), 'dp', scatter_dimension=1,...]
    pallas_call x0 -> x4, Pallas kernels: none -> 229 us  [the longest x1 130 us: experts(): pl.pallas_call(functools.partial(expert_kernel, n, plan), out_shape=jax.S...]
    all_to_all x2 -> x0, blocking collectives: 68.4 us -> none  [the longest x1 38.3 us: mixture(): lax.all_to_all(slot_rows, 'expert', split_axis=0, concat_axis=3, tiled=True)]
    dot_general x9 -> x10, matrix products: 83.6 us -> 16.2 us  [the longest x4 5.09 us: combine(): picked = jnp.dot(picks[k], arrived[model], preferred_element_type=f32)]
    all_to_all x1 -> x0, waiting for transfers between devices: 30.5 us -> none  [mixture(): lax.all_to_all(summed.reshape(1, slot_count, models, model_width), 'exper...]
    psum x2 -> x0, blocking collectives: 27.4 us -> none  [the longest x1 13.7 us: per_device(): lax.psum((policy_partial, reference_partial, policy_squares, reference_sq...]
    reshape x4 -> x0, local copies, waits for them, and re-layouts: 10.2 us -> none  [the longest x1 4.64 us: mixture(): local_rows = arrived_rows.reshape(slot_count, models, model_width)]
    all_to_all x2 -> x0, local copies, waits for them, and re-layouts: 8.37 us -> none  [the longest x1 4.65 us: mixture(): lax.all_to_all(local_rows, 'dp', split_axis=2, concat_axis=0, tiled=True)]
  transfers between devices with their start and end apart: 7 -> 0, of which waited for: 7 -> 0; matrix products, arithmetic and copies ran while one was open for 10% -> 0% of each run, Pallas kernels for 0% -> 0%
where the time goes in v1:
time: 274 us; the launch traced here: 270 us
  Pallas kernels  229 us (84%)
  matrix products  16.2 us (6%)
  other arithmetic  11.5 us (4%)
  local copies, waits for them, and re-layouts  10 us (4%)
  between operations  4.08 us (1%)
    pallas_call x1, Pallas kernels, experts(): pl.pallas_call(functools.partial(expert_kernel, n, plan), out_shape=jax.S...  130 us
    pallas_call x1, Pallas kernels, exit_exchange(): pl.pallas_call(functools.partial(exit_kernel, n, z), out_shape=(jax.Shape...  45.7 us
    pallas_call x1, Pallas kernels, entry_exchange(): pl.pallas_call(functools.partial(entry_kernel, n, z), out_shape=jax.Shape...  41.7 us
    pallas_call x1, Pallas kernels, small_exchange(): pl.pallas_call(functools.partial(small_kernel, n, z), out_shape=(jax.Shap...  10.7 us

profile of v1, /device:TPU:0, one launch (start us, length us, event | category | flops | bytes accessed | tf_op | source)
XLA Modules:
  0.0 270.3 jit_solution(4528791834768955045)
XLA Ops:
  0.7 0.8 iota_compare_fusion.14
  1.6 1.1 fusion.30
  2.7 1.1 fusion.31
  3.7 1.5 convolution_bitcast_fusion.1
  5.2 1.5 convolution_bitcast_fusion
  6.7 0.6 select_maximum_fusion.terms_ref
  7.6 0.8 copy.40
  8.9 0.6 pad.13.counts_ref
  9.5 10.7 %small_exchange.1 = (f32[4,16,128]{2,1,0:T(8,128)}, f32[8,8,128]{2,1,0:T(8,128)}) custom-call(f32[16,128]{1,0:T(8,128)} %select_maximum_fusion.terms_ref, f32[8,128]{1,0:T(8,128)} %pad.13.counts_ref), custom_call_target="tpu_custom_call" | custom-call | tf_op jit(solution)/shard_map/small_exchange/pallas_call | solution.py:68
  20.1 0.8 reduce_sum.149
  20.9 0.8 fusion.65
  21.7 0.6 reduce_max.36
  23.0 0.8 slice_convert_fusion
  24.3 0.7 select_reduce_fusion
  25.8 1.1 fusion.66
  27.0 0.7 maximum_bitcast_fusion
  28.2 0.6 pad.14.stats_ref
  29.7 1.7 convolution_convert_fusion.2.placed
  31.4 41.7 %entry_exchange.1 = bf16[2,768,512]{2,1,0:T(8,128)(2,1)S(1)} custom-call(bf16[384,2048]{1,0:T(8,128)(2,1)} %convolution_convert_fusion.2.placed), custom_call_target="tpu_custom_call" | custom-call | tf_op jit(solution)/shard_map/entry_exchange/pallas_call | solution.py:162
  73.1 1.3 broadcast_in_dim.42
  74.4 137.9 %while.11 = (s32[]{:T(128)}, bf16[2,768,512]{1,2,0:T(8,128)(2,1)}, s32[]{:T(128)}, bf16[2,768,512]{2,1,0:T(8,128)(2,1)S(1)}, bf16[512,8192]{1,0:T(8,128)(2,1)}, ...) while((s32[]{:T(128)}, bf16[2,768,512]{1,2,0:T(8,128)(2,1)}, ...), condition=%wide.region_9.10_spmd.clone, body=%wide.region_8.9_spmd.clone.sunk | while | flops 17115155456 | bytes 68969120 | solution.py:658
  74.5 0.8 eq.273
  75.6 2.2 fusion.80.rows_ref
  77.8 130.5 %experts.1 = bf16[2,320,512]{2,1,0:T(8,128)(2,1)} custom-call(bf16[2,320,512]{2,1,0:T(8,128)(2,1)} %fusion.80.rows_ref, bf16[512,8192]{1,0:T(8,128)(2,1)} %get-tuple-element.254.gate0, bf16[512,8192]{1,0:T(8,128)(2,1)} %get-tuple-element.255.up0, bf16[1024,4096]{1,0:T(8,128)(2,1)} %get-tuple-element.256.down0, bf16[512,8192]{1,0:T(8,128)(2,1)} %get-tuple-element.257.gate1, ...), custom_call_target="tpu_custom_call" | custom-call | flops 16106127360 | bytes 50331648 | tf_op jit(solution)/shard_map/while/body/experts/pallas_call | solution.py:532
  208.3 4.0 %bitcast_add_fusion.2 = bf16[2,768,512]{1,2,0:T(8,128)(2,1)} fusion(bf16[2,768,512]{1,2,0:T(8,128)(2,1)} %get-tuple-element.237, bf16[2,320,512]{2,1,0:T(8,128)(2,1)} %experts.1, s32[768]{0:T(1024)} %eq.273, s32[320]{0:T(512)} %copy-done.5), kind=kOutput, calls=%fused_computation.2.clone.1 | convolution fusion | flops 505135104 | bytes 3805440 | tf_op jit(solution)/shard_map/while/body/sr,mrd->msd/dot_general | solution.py:653
  212.3 2.6 copy.43.rows_ref
  214.9 45.7 %exit_exchange.1 = (bf16[2,384,1024]{2,1,0:T(8,128)(2,1)}, f32[8,8,128]{2,1,0:T(8,128)}) custom-call(bf16[2,768,512]{2,1,0:T(8,128)(2,1)} %copy.43.rows_ref, f32[8,128]{1,0:T(8,128)} %pad.14.stats_ref), custom_call_target="tpu_custom_call" | custom-call | tf_op jit(solution)/shard_map/exit_exchange/pallas_call | solution.py:268
  260.6 0.9 slice_reduce_fusion
  261.5 0.6 multiply_reduce_fusion.1
  264.1 1.5 convolution_multiply_fusion.1
  265.6 2.2 fusion.16
  268.2 1.1 fusion.15
  (84 shorter events, 4.8 us)
Async XLA Ops:
  0.6 28.4 %copy-start.12 = (s32[128,2]{0,1:T(2,128)S(1)}, s32[128,2]{0,1:T(2,128)}, u32[]{:S(2)}) copy-start(s32[128,2]{0,1:T(2,128)} %param.29) | copy-start | bytes 3076
  0.6 28.5 %copy-start.1 = (bf16[128,1024]{1,0:T(8,128)(2,1)S(1)}, bf16[128,1024]{1,0:T(8,128)(2,1)}, u32[]{:S(2)}) copy-start(bf16[128,1024]{1,0:T(8,128)(2,1)} %param.18) | copy-start | bytes 786436
  0.7 28.5 %copy-start.2 = (bf16[128,1024]{1,0:T(8,128)(2,1)S(1)}, bf16[128,1024]{1,0:T(8,128)(2,1)}, u32[]{:S(2)}) copy-start(bf16[128,1024]{1,0:T(8,128)(2,1)} %param.17) | copy-start | bytes 786436
  0.7 28.4 %copy-start.8 = (f32[1024]{0:T(1024)S(1)}, f32[1024]{0:T(1024)}, u32[]{:S(2)}) copy-start(f32[1024]{0:T(1024)} %param.20) | copy-start | bytes 12292
  0.7 28.4 %copy-start.9 = (f32[1024]{0:T(1024)S(1)}, f32[1024]{0:T(1024)}, u32[]{:S(2)}) copy-start(f32[1024]{0:T(1024)} %param.19) | copy-start | bytes 12292
  1.6 27.7 %copy-start.17 = (f32[128]{0:T(128)}, f32[128]{0:T(128)S(1)}, u32[]{:S(2)}) copy-start(f32[128]{0:T(128)S(1)} %convert_element_type.101) | copy-start | bytes 1540
  21.7 2.6 copy-start.23
  29.1 0.5 copy-start.13
  29.1 0.6 copy-start.15
  74.4 1.2 copy-start.3
  74.4 1.2 copy-start.6
  74.4 1.2 copy-start.10
  74.4 1.2 copy-start.5
  208.3 4.0 %copy-start.4 = (bf16[2,768,512]{2,1,0:T(8,128)(2,1)S(1)}, bf16[2,768,512]{2,1,0:T(8,128)(2,1)}, u32[]{:S(2)}) copy-start(bf16[2,768,512]{2,1,0:T(8,128)(2,1)} %copy-done.3) | copy-start | bytes 4718596 | tf_op jit(solution)/shard_map/while
  208.3 4.0 %copy-start.7 = (s32[8]{0:T(128)S(1)}, s32[8]{0:T(128)}, u32[]{:S(2)}) copy-start(s32[8]{0:T(128)} %copy-done.6) | copy-start | bytes 100 | tf_op jit(solution)/shard_map/while
  208.3 4.0 %copy-start.11 = (s32[8]{0:T(128)S(1)}, s32[8]{0:T(128)}, u32[]{:S(2)}) copy-start(s32[8]{0:T(128)} %copy-done.10) | copy-start | bytes 100 | tf_op jit(solution)/shard_map/while
  214.9 46.6 %copy-start.24 = (s32[4]{0:T(128)S(1)}, s32[4]{0:T(128)}, u32[]{:S(2)}) copy-start(s32[4]{0:T(128)} %copy-done.23) | copy-start | bytes 52
  214.9 49.1 %copy-start.16 = (s32[128]{0:T(128)S(1)}, s32[128]{0:T(128)}, u32[]{:S(2)}) copy-start(s32[128]{0:T(128)} %copy-done.15) | copy-start | bytes 1540
  214.9 49.1 %copy-start.22 = (f32[128]{0:T(128)S(1)}, f32[128]{0:T(128)}, u32[]{:S(2)}) copy-start(f32[128]{0:T(128)} %get-tuple-element.139) | copy-start | bytes 1540
  214.9 50.6 %copy-start.14 = (s32[128]{0:T(128)S(1)}, s32[128]{0:T(128)}, u32[]{:S(2)}) copy-start(s32[128]{0:T(128)} %copy-done.13) | copy-start | bytes 1540
  214.9 50.6 %copy-start.18 = (f32[128]{0:T(128)S(1)}, f32[128]{0:T(128)}, u32[]{:S(2)}) copy-start(f32[128]{0:T(128)} %copy-done.17) | copy-start | bytes 1540
  214.9 50.6 %copy-start.20 = (f32[128]{0:T(128)S(1)}, f32[128]{0:T(128)}, u32[]{:S(2)}) copy-start(f32[128]{0:T(128)} %get-tuple-element.138) | copy-start | bytes 1540
  260.6 7.2 %copy-start = (bf16[2,384,1024]{2,1,0:T(8,128)(2,1)S(1)}, bf16[2,384,1024]{2,1,0:T(8,128)(2,1)}, u32[]{:S(2)}) copy-start(bf16[2,384,1024]{2,1,0:T(8,128)(2,1)} %get-tuple-element.70) | copy-start | bytes 4718596
  260.6 7.2 %copy-start.21 = (f32[128]{0:T(128)S(1)}, f32[128]{0:T(128)}, u32[]{:S(2)}) copy-start(f32[128]{0:T(128)} %get-tuple-element.141) | copy-start | bytes 1540
  265.6 2.6 copy-start.19
